TPU v7x, 32 devices: a whole 2x2x4 slice. The times are simulated.
32 devices in a mesh: row: 16 (over z, x, core), chan: 2 (over y).
Axes of the slice: x: 2, y: 2, z: 4, core: 2. Of those that a mesh axis runs over, the one named last changes fastest.
Arguments:
- pair_rep: float32 [256, 256, 128], P('row', 'chan'), may hold values from -630 to 630
- residue_mask: int32 [256], replicated, may hold values from 0 to 1, as said below
- norm_gain: float32 [128], replicated, may hold values from 0.5 to 1.5
- norm_shift: float32 [128], replicated, may hold values from -3 to 3
- proj_weight: float32 [128, 512], replicated, may hold values from -4 to 4
- gate_shift: float32 [128], replicated, may hold values from -4 to 4
- bias_weight: float32 [128, 4], replicated, may hold values from -0.5 to 0.5
- out_weight: float32 [128, 128], replicated, may hold values from -0.5 to 0.5
Outputs:
- update: float32 [256, 256, 128], P('row', 'chan')
Inputs may be any that keep to these rules, and one draw needn't show every extreme that they name: `residue_mask`: residue 0 is always valid.
All inputs are finite; a program needn't handle non-finite values.
Results may differ from a plain program's by a relative error of at most 0.012.
Values may be sent and summed in bfloat16 or wider, within the bound.
A program may use at most 64 MiB of HBM per device.

v0:
```python
import functools
import math

import jax
import jax.numpy as jnp
from jax import lax
from jax.experimental import pallas as pl
from jax.experimental.pallas import tpu as pltpu
from jax.sharding import PartitionSpec as P

HEADS = 4
MESH = pl.DeviceIdType.MESH
NT = (((1,), (1,)), ((), ()))
NEVER = -1e30


def halves(value):
    high = value.astype(jnp.bfloat16)
    return high, (value - high.astype(jnp.float32)).astype(jnp.bfloat16)


def kernel(
    chans,
    group,
    x_ref,
    mask_ref,
    gain_ref,
    shift_ref,
    proj_ref,
    gate_ref,
    bw_ref,
    ow_ref,
    out_ref,
    xall,
    blocks,
    stage,
    own_bias,
    bias,
    w_own,
    w_kv,
    w_out,
    xlow,
    queries,
    gates,
    keys,
    values,
    result,
    x_send,
    x_recv,
    far_send,
    far_recv,
    near_send,
    near_recv,
    out_sem,
):
    rows, span, width = x_ref.shape
    total = chans * span
    head_dim = width // HEADS
    r = lax.axis_index("row")
    c = lax.axis_index("chan")
    hi = r // group
    lo = r % group
    is_home = (hi == c).astype(jnp.int32)

    barrier = pltpu.get_barrier_semaphore()
    for d in range(1, chans):
        pl.semaphore_signal(barrier, inc=1, device_id=(r, (c + d) % chans), device_id_type=MESH)
    for s in range(chans):

        @pl.when(jnp.logical_or(hi != c, c != s))
        def _():
            pl.semaphore_signal(barrier, inc=1, device_id=(c * group + lo, s), device_id_type=MESH)

    for d in range(1, group):
        pl.semaphore_signal(
            barrier, inc=1, device_id=(hi * group + (lo + d) % group, c), device_id_type=MESH
        )

    exp_scale = math.log2(math.e)
    proj_high, proj_low = halves(proj_ref[...])
    w_own[:width] = proj_high
    w_own[width : 2 * width] = proj_high
    w_own[2 * width :] = proj_low
    w_kv[:width] = proj_high[:, width : 3 * width]
    w_kv[width:] = proj_low[:, width : 3 * width]
    out_high, out_low = halves(ow_ref[...])
    w_out[:width] = out_high
    w_out[width : 2 * width] = out_high
    w_out[2 * width :] = out_low
    bw_high, bw_low = halves(bw_ref[...])
    bw_t = jnp.concatenate([bw_high, bw_high, bw_low], axis=1)
    gain = gain_ref[...].reshape(1, 1, width)
    shift = shift_ref[...].reshape(1, 1, width)

    step = 4 if rows % 4 == 0 else 1

    def norm_rows(n, carry):
        x = x_ref[pl.ds(n * step, step)]
        centered = x - jnp.mean(x, axis=-1, keepdims=True)
        variance = jnp.mean(centered * centered, axis=-1, keepdims=True)
        high, low = halves(centered * lax.rsqrt(variance + 1e-05) * gain + shift)
        for m in range(step):
            xall[n * step + m, c] = high[m]
            xlow[n * step + m] = low[m]
            local = lax.dot_general(
                bw_t,
                jnp.concatenate([high[m], low[m], high[m]], axis=1),
                NT,
                preferred_element_type=jnp.float32,
            )
            stage[:, n * step + m, :] = local[:HEADS] * exp_scale
        return carry

    lax.fori_loop(0, rows // step, norm_rows, 0)
    own_bias[...] = stage[...].astype(jnp.bfloat16)

    @pl.when(hi == c)
    def _():
        blocks[lo, c] = stage[...].astype(jnp.bfloat16)

    pl.semaphore_wait(barrier, 2 * chans - 1 - is_home + group - 1)

    def far_copy(g, source):
        return pltpu.make_async_remote_copy(
            src_ref=own_bias,
            dst_ref=blocks.at[lo, source],
            send_sem=far_send.at[g],
            recv_sem=far_recv.at[source],
            device_id=(g * group + lo, hi),
            device_id_type=MESH,
        )

    for g in range(chans):

        @pl.when(jnp.logical_or(hi != c, hi != g))
        def _():
            far_copy(g, c).start()

    def x_copy(i, d, source):
        return pltpu.make_async_remote_copy(
            src_ref=xall.at[i, source],
            dst_ref=xall.at[i, source],
            send_sem=x_send.at[d - 1, i],
            recv_sem=x_recv.at[d - 1, i],
            device_id=(r, (c + d) % chans),
            device_id_type=MESH,
        )

    def send_row(i, carry):
        for d in range(1, chans):
            x_copy(i, d, c).start()
        return carry

    early = rows // 4
    lax.fori_loop(0, early, send_row, 0)

    scaling = exp_scale / math.sqrt(head_dim)

    def project_own(i, carry):
        high = xall[i, c]
        full = jnp.dot(
            jnp.concatenate([high, xlow[i], high], axis=1),
            w_own[...],
            preferred_element_type=jnp.float32,
        )
        queries[i] = (full[:, :width] * scaling).astype(jnp.bfloat16)
        keys[i, c] = full[:, width : 2 * width].astype(jnp.bfloat16)
        values[i, c, :, :width] = full[:, 2 * width : 3 * width].astype(jnp.bfloat16)
        gates[i] = jax.nn.sigmoid(full[:, 3 * width :] + gate_ref[...])
        for s in range(chans):
            values[i, s, :, width:] = jnp.ones((span, width), jnp.bfloat16)
        return carry

    lax.fori_loop(0, rows, project_own, 0)

    for s in range(chans):

        @pl.when(jnp.logical_or(hi != c, c != s))
        def _():
            far_copy(s, s).wait_recv()

    def near_copy(d, source):
        return pltpu.make_async_remote_copy(
            src_ref=blocks.at[source],
            dst_ref=blocks.at[source],
            send_sem=near_send.at[d - 1],
            recv_sem=near_recv.at[d - 1],
            device_id=(hi * group + (lo + d) % group, c),
            device_id_type=MESH,
        )

    for d in range(1, group):
        near_copy(d, lo).start()
    lax.fori_loop(early, rows, send_row, 0)

    def project_other(i, carry):
        for d in range(1, chans):
            source = (c + chans - d) % chans
            x_copy(i, d, source).wait_recv()
            other = xall[i, source]
            kv = jnp.dot(
                jnp.concatenate([other, other], axis=1),
                w_kv[...],
                preferred_element_type=jnp.float32,
            )
            keys[i, source] = kv[:, :width].astype(jnp.bfloat16)
            values[i, source, :, :width] = kv[:, width:].astype(jnp.bfloat16)
        return carry

    lax.fori_loop(0, early, project_other, 0)

    for d in range(1, group):
        near_copy(d, (lo + group - d) % group).wait_recv()

    valid = mask_ref[...] > 0
    for s in range(chans):
        keep = valid[:, s * span : (s + 1) * span].reshape(1, 1, span)
        for h in range(HEADS):
            part = blocks[:, s, h].astype(jnp.float32)
            bias[h, :, :, s * span : (s + 1) * span] = jnp.where(keep, part, NEVER)

    lane = lax.broadcasted_iota(jnp.int32, (span, width), 1) // head_dim

    def out_copy(i):
        return pltpu.make_async_copy(result.at[i], out_ref.at[i], out_sem.at[i])

    def attend(i, carry):
        query = queries[i]
        key = keys[i].reshape(total, width)
        value = values[i].reshape(total, 2 * width)
        top = jnp.zeros((span, width), jnp.float32)
        norm = jnp.zeros((span, width), jnp.float32)
        for h in range(HEADS):
            mine = jnp.where(lane == h, query, jnp.zeros_like(query))
            scores = lax.dot_general(mine, key, NT, preferred_element_type=jnp.float32)
            scores = scores + bias[h].reshape(span, total)
            peak = jnp.max(scores, axis=-1, keepdims=True)
            weights = jnp.exp2(scores - peak).astype(jnp.bfloat16)
            both = jnp.dot(weights, value, preferred_element_type=jnp.float32)
            top = jnp.where(lane == h, both[:, :width], top)
            norm = jnp.where(lane == h, both[:, width:], norm)
        high, low = halves(gates[i] * (top / norm))
        result[i] = jnp.dot(
            jnp.concatenate([high, low, high], axis=1),
            w_out[...],
            preferred_element_type=jnp.float32,
        )
        out_copy(i).start()
        return carry

    def attend_ahead(i, carry):
        project_other(i + early, carry)
        return attend(i, carry)

    lax.fori_loop(0, rows - early, attend_ahead, 0)
    lax.fori_loop(rows - early, rows, attend, 0)

    for g in range(chans):

        @pl.when(jnp.logical_or(hi != c, hi != g))
        def _():
            far_copy(g, c).wait_send()

    for d in range(1, group):
        near_copy(d, lo).wait_send()

    def finish(i, carry):
        for d in range(1, chans):
            x_copy(i, d, c).wait_send()
        out_copy(i).wait()
        return carry

    lax.fori_loop(0, rows, finish, 0)


def body(
    chans,
    pair_rep,
    residue_mask,
    norm_gain,
    norm_shift,
    proj_weight,
    gate_shift,
    bias_weight,
    out_weight,
):
    rows, span, width = pair_rep.shape
    group = span // rows
    total = chans * span
    vmem = pl.BlockSpec(memory_space=pltpu.VMEM)
    half = jnp.bfloat16
    full = jnp.float32
    return pl.pallas_call(
        functools.partial(kernel, chans, group),
        out_shape=jax.ShapeDtypeStruct((rows, span, width), full),
        in_specs=[vmem] * 8,
        out_specs=pl.BlockSpec(memory_space=pl.ANY),
        scratch_shapes=[
            pltpu.VMEM((rows, chans, span, width), half),
            pltpu.VMEM((group, chans, HEADS, rows, span), half),
            pltpu.VMEM((HEADS, rows, span), full),
            pltpu.VMEM((HEADS, rows, span), half),
            pltpu.VMEM((HEADS, group, rows, total), full),
            pltpu.VMEM((3 * width, 4 * width), half),
            pltpu.VMEM((2 * width, 2 * width), half),
            pltpu.VMEM((3 * width, width), half),
            pltpu.VMEM((rows, span, width), half),
            pltpu.VMEM((rows, span, width), half),
            pltpu.VMEM((rows, span, width), full),
            pltpu.VMEM((rows, chans, span, width), half),
            pltpu.VMEM((rows, chans, span, 2 * width), half),
            pltpu.VMEM((rows, span, width), full),
            pltpu.SemaphoreType.DMA((chans - 1, rows)),
            pltpu.SemaphoreType.DMA((chans - 1, rows)),
            pltpu.SemaphoreType.DMA((chans,)),
            pltpu.SemaphoreType.DMA((chans,)),
            pltpu.SemaphoreType.DMA((group - 1,)),
            pltpu.SemaphoreType.DMA((group - 1,)),
            pltpu.SemaphoreType.DMA((rows,)),
        ],
        compiler_params=pltpu.CompilerParams(
            collective_id=0, has_side_effects=True, vmem_limit_bytes=56 * 1024 * 1024
        ),
    )(
        pair_rep,
        residue_mask.reshape(1, total),
        norm_gain.reshape(1, width),
        norm_shift.reshape(1, width),
        proj_weight,
        gate_shift.reshape(1, width),
        bias_weight.T,
        out_weight,
    )


def solution(mesh):
    return jax.shard_map(
        functools.partial(body, mesh.shape["chan"]),
        mesh=mesh,
        in_specs=(P("row", "chan", None), P(), P(), P(), P(), P(), P(), P()),
        out_specs=P("row", "chan", None),
        check_vma=False,
    )
```

profile of v0, /device:TPU:0, one launch (start us, length us, event | category | flops | bytes accessed | tf_op | source)
XLA Modules:
  0.0 29.8 jit_solution(4958884700149232248)
XLA Ops:
  0.0 27.5 %shard_map.82 = f32[16,128,128]{2,1,0:T(8,128)} custom-call(f32[16,128,128]{2,1,0:T(8,128)} %x_ref.1, s32[1,256]{1,0:T(1,128)} %bitcast.6, f32[1,128]{1,0:T(1,128)} %bitcast.7, f32[1,128]{1,0:T(1,128)} %bitcast.8, f32[128,512]{1,0:T(8,128)} %proj_ref.1, f32[1,128]{1,0:T(1,128)} %bitcast.9, f32[4,128]{1,0:T(4,128)} %bitcast.5, f32[128,128]{1,0:T(8,128)} %ow_ref.1), custom_call_target="tpu_custom_call" | custom-call | tf_op jit(solution)/shard_map/pallas_call | solution.py:293
  27.5 2.3 %copy.10 = f32[16,128,128]{2,1,0:T(8,128)} copy(f32[16,128,128]{2,1,0:T(8,128)} %shard_map.82) | data formatting | bytes 2097152
where the time goes:
time: 30 us; the launch traced here: 29.8 us
  Pallas kernels  27.5 us (92%)
  local copies, waits for them, and re-layouts  2.3 us (8%)
    pallas_call x1, Pallas kernels, body(): pl.pallas_call(functools.partial(kernel, chans, group), out_shape=jax.Sha...  27.5 us
    unnamed x1, local copies, waits for them, and re-layouts  2.3 us

commit v1 on v0

v1 whole, which is shorter than its diff:
```python
import functools
import math

import jax
import jax.numpy as jnp
from jax import lax
from jax.experimental import pallas as pl
from jax.experimental.pallas import tpu as pltpu
from jax.sharding import PartitionSpec as P

HEADS = 4
MESH = pl.DeviceIdType.MESH
NT = (((1,), (1,)), ((), ()))
NEVER = -1e30
LOG2E = math.log2(math.e)


def halves(value):
    high = value.astype(jnp.bfloat16)
    return high, (value - high.astype(jnp.float32)).astype(jnp.bfloat16)


def kernel(
    chans,
    group,
    x_hbm,
    mask_hbm,
    gain_hbm,
    shift_hbm,
    proj_hbm,
    gate_hbm,
    bw_hbm,
    ow_hbm,
    out_ref,
    x_ref,
    mask_ref,
    gain_ref,
    shift_ref,
    proj_ref,
    gate_ref,
    bw_ref,
    ow_ref,
    xall,
    blocks,
    stage,
    own_bias,
    bias,
    w_own,
    w_out,
    queries,
    gates,
    keys,
    values,
    scores,
    peaks,
    gated,
    load_sem,
    chunk_sem,
    x_send,
    x_recv,
    far_send,
    far_recv,
    near_send,
    near_recv,
):
    rows, span, width = x_ref.shape
    total = chans * span
    head_dim = width // HEADS
    r = lax.axis_index("row")
    c = lax.axis_index("chan")
    hi = r // group
    lo = r % group
    is_home = (hi == c).astype(jnp.int32)
    step = 4 if rows % 4 == 0 else 1
    early = max(rows // 8, 1)
    last = rows // 4

    barrier = pltpu.get_barrier_semaphore()
    for d in range(1, chans):
        pl.semaphore_signal(barrier, inc=1, device_id=(r, (c + d) % chans), device_id_type=MESH)
    for s in range(chans):

        @pl.when(jnp.logical_or(hi != c, c != s))
        def _():
            pl.semaphore_signal(barrier, inc=1, device_id=(c * group + lo, s), device_id_type=MESH)

    for d in range(1, group):
        pl.semaphore_signal(
            barrier, inc=1, device_id=(hi * group + (lo + d) % group, c), device_id_type=MESH
        )

    loads = [
        pltpu.make_async_copy(source, target, load_sem.at[k])
        for k, (source, target) in enumerate(
            [
                (gain_hbm, gain_ref),
                (shift_hbm, shift_ref),
                (bw_hbm, bw_ref),
                (proj_hbm, proj_ref),
                (gate_hbm, gate_ref),
                (ow_hbm, ow_ref),
                (mask_hbm, mask_ref),
            ]
        )
    ]
    spans = (pl.ds(0, early), pl.ds(early, rows - early))
    chunks = [
        pltpu.make_async_copy(x_hbm.at[here], x_ref.at[here], chunk_sem.at[k])
        for k, here in enumerate(spans)
    ]
    for copy in loads[:3] + chunks + loads[3:]:
        copy.start()
    for copy in loads[:3]:
        copy.wait()
    gain = gain_ref[...].reshape(1, 1, width)
    shift = shift_ref[...].reshape(1, 1, width)
    bw_both = jnp.concatenate(halves(bw_ref[...] * LOG2E), axis=0)

    def norm_rows(first, count):
        x = x_ref[first : first + count]
        centered = x - jnp.mean(x, axis=-1, keepdims=True)
        variance = jnp.mean(centered * centered, axis=-1, keepdims=True)
        high = (centered * lax.rsqrt(variance + 1e-05) * gain + shift).astype(jnp.bfloat16)
        for m in range(count):
            xall[first + m, c] = high[m]
        both = lax.dot_general(
            bw_both,
            high.reshape(count * span, width),
            NT,
            preferred_element_type=jnp.float32,
        )
        local = both[:HEADS] + both[HEADS:]
        for m in range(count):
            stage[:, first + m, :] = local[:, m * span : (m + 1) * span]

    def x_copy(i, d, source):
        return pltpu.make_async_remote_copy(
            src_ref=xall.at[i, source],
            dst_ref=xall.at[i, source],
            send_sem=x_send.at[d - 1, i],
            recv_sem=x_recv.at[d - 1, i],
            device_id=(r, (c + d) % chans),
            device_id_type=MESH,
        )

    def send_row(i, carry):
        for d in range(1, chans):
            x_copy(i, d, c).start()
        return carry

    with jax.named_scope("norm0"):
        chunks[0].wait()
        norm_rows(0, early)
    with jax.named_scope("barrier"):
        pl.semaphore_wait(barrier, 2 * chans - 1 - is_home + group - 1)
    lax.fori_loop(0, early, send_row, 0)

    with jax.named_scope("norm1"):
        chunks[1].wait()
        for first in range(early, rows, early):
            norm_rows(first, min(early, rows - first))
        own_bias[...] = stage[...].astype(jnp.bfloat16)

        @pl.when(hi == c)
        def _():
            blocks[lo, c] = stage[...].astype(jnp.bfloat16)

    def far_copy(g, source):
        return pltpu.make_async_remote_copy(
            src_ref=own_bias,
            dst_ref=blocks.at[lo, source],
            send_sem=far_send.at[g],
            recv_sem=far_recv.at[source],
            device_id=(g * group + lo, hi),
            device_id_type=MESH,
        )

    for g in range(chans):

        @pl.when(jnp.logical_or(hi != c, hi != g))
        def _():
            far_copy(g, c).start()

    def near_copy(d, source, part):
        return pltpu.make_async_remote_copy(
            src_ref=blocks.at[source, part],
            dst_ref=blocks.at[source, part],
            send_sem=near_send.at[d - 1, part],
            recv_sem=near_recv.at[d - 1, part],
            device_id=(hi * group + (lo + d) % group, c),
            device_id_type=MESH,
        )

    @pl.when(hi == c)
    def _():
        for d in range(1, group):
            near_copy(d, lo, c).start()

    lax.fori_loop(early, rows, send_row, 0)

    loads[3].wait()
    loads[4].wait()
    proj_high, proj_low = halves(proj_ref[...])
    w_own[:width] = proj_high
    w_own[width:] = proj_low
    scaling = LOG2E / math.sqrt(head_dim)

    def project_own(n, carry):
        here = pl.ds(n * step, step)
        high = xall[here, c].reshape(step * span, width)
        full = jnp.dot(
            jnp.concatenate([high, high], axis=1), w_own[...], preferred_element_type=jnp.float32
        )
        shape = (step, span, width)
        queries[here] = (full[:, :width] * scaling).astype(jnp.bfloat16).reshape(shape)
        keys[here, c] = full[:, width : 2 * width].astype(jnp.bfloat16).reshape(shape)
        values[here, c] = full[:, 2 * width : 3 * width].astype(jnp.bfloat16).reshape(shape)
        half = 0.5 * (full[:, 3 * width :] + gate_ref[...])
        gates[here] = (0.5 * jnp.tanh(half) + 0.5).reshape(shape)
        return carry

    with jax.named_scope("project_own"):
        lax.fori_loop(0, rows // step, project_own, 0)

    loads[5].wait()
    loads[6].wait()
    out_high, out_low = halves(ow_ref[...])
    w_out[:width] = out_high
    w_out[width:] = out_low

    with jax.named_scope("far_wait"):
        for k in range(chans):
            part = (c + k) % chans

            @pl.when(jnp.logical_or(hi != c, k > 0))
            def _():
                far_copy(part, part).wait_recv()
                for d in range(1, group):
                    near_copy(d, lo, part).start()

    def project_other(i):
        for d in range(1, chans):
            source = (c + chans - d) % chans
            with jax.named_scope("x_wait"):
                x_copy(i, d, source).wait_recv()
            other = xall[i, source]
            kv = jnp.dot(
                jnp.concatenate([other, other], axis=1),
                w_own[:, width : 3 * width],
                preferred_element_type=jnp.float32,
            )
            keys[i, source] = kv[:, :width].astype(jnp.bfloat16)
            values[i, source] = kv[:, width:].astype(jnp.bfloat16)

    with jax.named_scope("kv_first"):
        for i in range(min(4, rows - last)):
            project_other(i)

    with jax.named_scope("near_wait"):
        for d in range(1, group):
            for part in range(chans):
                near_copy(d, (lo + group - d) % group, part).wait_recv()

    with jax.named_scope("bias_prep"):
        valid = mask_ref[...] > 0
        for s in range(chans):
            keep = valid[:, s * span : (s + 1) * span].reshape(1, 1, span)
            for h in range(HEADS):
                part = blocks[:, s, h].astype(jnp.float32)
                bias[h, :, s * span : (s + 1) * span] = jnp.where(keep, part, NEVER).reshape(
                    span, span
                )

    tall = (HEADS * span, width)
    lane = lax.broadcasted_iota(jnp.int32, (span, width), 1) // head_dim
    own_lane = lax.broadcasted_iota(jnp.int32, tall, 1) // head_dim
    own_head = lax.broadcasted_iota(jnp.int32, tall, 0) // span

    def score(i, slot):
        mine = jnp.concatenate([queries[i]] * HEADS, axis=0)
        mine = jnp.where(own_lane == own_head, mine, jnp.zeros_like(mine))
        part = lax.dot_general(
            mine, keys[i].reshape(total, width), NT, preferred_element_type=jnp.float32
        )
        part = part + bias[...].reshape(HEADS * span, total)
        scores[slot] = part
        peaks[slot] = jnp.broadcast_to(jnp.max(part, axis=-1, keepdims=True), tall)

    def attend(i, slot):
        peak = jnp.concatenate([peaks[slot]] * (total // width), axis=1)
        weights = jnp.exp2(scores[slot] - peak).astype(jnp.bfloat16)
        value = jnp.concatenate(
            [values[i].reshape(total, width), jnp.ones((total, width), jnp.bfloat16)], axis=1
        )
        both = jnp.dot(weights, value, preferred_element_type=jnp.float32)
        top = both[:span, :width]
        norm = both[:span, width:]
        for h in range(1, HEADS):
            here = slice(h * span, (h + 1) * span)
            top = jnp.where(lane == h, both[here, :width], top)
            norm = jnp.where(lane == h, both[here, width:], norm)
        gated[slot] = (gates[i] * (top / norm)).astype(jnp.bfloat16)

    def finish_row(i, slot):
        mine = gated[slot]
        out_ref[i] = jnp.dot(
            jnp.concatenate([mine, mine], axis=1), w_out[...], preferred_element_type=jnp.float32
        )

    body = rows - last
    pairs = [list(range(n, min(n + 2, body))) for n in range(0, body, 2)]

    def slot(i):
        return i % 4

    with jax.named_scope("score0"):
        for i in pairs[0]:
            score(i, slot(i))
    for n, pair in enumerate(pairs):
        with jax.named_scope(f"pair{n}"):
            if n + 2 < len(pairs):
                for i in pairs[n + 2]:
                    project_other(i)
            for u, i in enumerate(pair):
                if n > 0:
                    finish_row(pairs[n - 1][u], slot(pairs[n - 1][u]))
                if n + 1 < len(pairs) and u < len(pairs[n + 1]):
                    score(pairs[n + 1][u], slot(pairs[n + 1][u]))
                attend(i, slot(i))
    pending = list(pairs[-1])
    waiting = None
    for i in range(body, rows):
        with jax.named_scope(f"row{i}"):
            project_other(i)
            score(i, slot(i))
            for k in pending:
                finish_row(k, slot(k))
            pending = []
            if waiting is not None:
                attend(waiting, slot(waiting))
                pending = [waiting]
            waiting = i
    with jax.named_scope("tail"):
        for k in pending:
            finish_row(k, slot(k))
        attend(waiting, slot(waiting))
        finish_row(waiting, slot(waiting))

    with jax.named_scope("finish"):
        for g in range(chans):

            @pl.when(jnp.logical_or(hi != c, hi != g))
            def _():
                far_copy(g, c).wait_send()

        for d in range(1, group):
            for part in range(chans):
                near_copy(d, lo, part).wait_send()

        def sent(i, carry):
            for d in range(1, chans):
                x_copy(i, d, c).wait_send()
            return carry

        lax.fori_loop(0, rows, sent, 0)


def body(
    chans,
    pair_rep,
    residue_mask,
    norm_gain,
    norm_shift,
    proj_weight,
    gate_shift,
    bias_weight,
    out_weight,
):
    rows, span, width = pair_rep.shape
    group = span // rows
    total = chans * span
    half = jnp.bfloat16
    full = jnp.float32
    return pl.pallas_call(
        functools.partial(kernel, chans, group),
        out_shape=jax.ShapeDtypeStruct((rows, span, width), full),
        in_specs=[pl.BlockSpec(memory_space=pltpu.HBM)] * 8,
        out_specs=pl.BlockSpec(memory_space=pltpu.VMEM),
        scratch_shapes=[
            pltpu.VMEM((rows, span, width), full),
            pltpu.VMEM((1, total), jnp.int32),
            pltpu.VMEM((1, width), full),
            pltpu.VMEM((1, width), full),
            pltpu.VMEM((width, 4 * width), full),
            pltpu.VMEM((1, width), full),
            pltpu.VMEM((HEADS, width), full),
            pltpu.VMEM((width, width), full),
            pltpu.VMEM((rows, chans, span, width), half),
            pltpu.VMEM((group, chans, HEADS, rows, span), half),
            pltpu.VMEM((HEADS, rows, span), full),
            pltpu.VMEM((HEADS, rows, span), half),
            pltpu.VMEM((HEADS, span, total), full),
            pltpu.VMEM((2 * width, 4 * width), half),
            pltpu.VMEM((2 * width, width), half),
            pltpu.VMEM((rows, span, width), half),
            pltpu.VMEM((rows, span, width), full),
            pltpu.VMEM((rows, chans, span, width), half),
            pltpu.VMEM((rows, chans, span, width), half),
            pltpu.VMEM((4, HEADS * span, total), full),
            pltpu.VMEM((4, HEADS * span, width), full),
            pltpu.VMEM((4, span, width), half),
            pltpu.SemaphoreType.DMA((7,)),
            pltpu.SemaphoreType.DMA((2,)),
            pltpu.SemaphoreType.DMA((chans - 1, rows)),
            pltpu.SemaphoreType.DMA((chans - 1, rows)),
            pltpu.SemaphoreType.DMA((chans,)),
            pltpu.SemaphoreType.DMA((chans,)),
            pltpu.SemaphoreType.DMA((group - 1, chans)),
            pltpu.SemaphoreType.DMA((group - 1, chans)),
        ],
        compiler_params=pltpu.CompilerParams(
            collective_id=0, has_side_effects=True, vmem_limit_bytes=(16 + 6 * chans) * 1024 * 1024
        ),
    )(
        *(
            pltpu.with_memory_space_constraint(operand, pltpu.HBM)
            for operand in (
                pair_rep,
                residue_mask.reshape(1, total),
                norm_gain.reshape(1, width),
                norm_shift.reshape(1, width),
                proj_weight,
                gate_shift.reshape(1, width),
                bias_weight.T,
                out_weight,
            )
        )
    )


def solution(mesh):
    return jax.shard_map(
        functools.partial(body, mesh.shape["chan"]),
        mesh=mesh,
        in_specs=(P("row", "chan", None), P(), P(), P(), P(), P(), P(), P()),
        out_specs=P("row", "chan", None),
        check_vma=False,
    )
```

time: 30 us -> 21.4 us (0.71)
  Pallas kernels: 27.5 us -> 20.3 us
  local copies, waits for them, and re-layouts: 2.3 us -> 0.97 us
    pallas_call x1, Pallas kernels: 27.5 us -> 20.3 us  [body(): pl.pallas_call(functools.partial(kernel, chans, group), out_shape=jax.Sha...]
    unnamed x1, local copies, waits for them, and re-layouts: 2.3 us -> 0.97 us
where the time goes in v1:
time: 21.4 us; the launch traced here: 21.3 us
  Pallas kernels  20.3 us (95%)
  local copies, waits for them, and re-layouts  0.97 us (5%)
    pallas_call x1, Pallas kernels, body(): pl.pallas_call(functools.partial(kernel, chans, group), out_shape=jax.Sha...  20.3 us
    unnamed x1, local copies, waits for them, and re-layouts  0.97 us

profile of v1, /device:TPU:0, one launch (start us, length us, event | category | flops | bytes accessed | tf_op | source)
XLA Modules:
  0.0 21.3 jit_solution(7784589351676204832)
XLA Ops:
  0.0 20.3 %shard_map.82 = f32[16,128,128]{2,1,0:T(8,128)S(1)} custom-call(f32[16,128,128]{2,1,0:T(8,128)} %x_hbm.1, s32[1,256]{1,0:T(1,128)} %bitcast.6, f32[1,128]{1,0:T(1,128)} %bitcast.7, f32[1,128]{1,0:T(1,128)} %bitcast.8, f32[128,512]{1,0:T(8,128)} %proj_hbm.1, f32[1,128]{1,0:T(1,128)} %bitcast.9, f32[4,128]{1,0:T(4,128)} %bitcast.5, f32[128,128]{1,0:T(8,128)} %ow_hbm.1), custom_call_target="tpu_custom_call" | custom-call | tf_op jit(solution)/shard_map/pallas_call | solution.py:384
  20.3 1.0 %copy.10 = f32[16,128,128]{2,1,0:T(8,128)} copy(f32[16,128,128]{2,1,0:T(8,128)S(1)} %shard_map.82) | data formatting | bytes 2097152

commit v2 on v1

--- a/solution.py
+++ b/solution.py
@@ -9,6 +9,9 @@
 from jax.sharding import PartitionSpec as P
 
 HEADS = 4
+MIDDLE = 3
+BATCH = 2
+AHEAD = 5
 MESH = pl.DeviceIdType.MESH
 NT = (((1,), (1,)), ((), ()))
 NEVER = -1e30
@@ -62,6 +65,8 @@
     far_recv,
     near_send,
     near_recv,
+    ready,
+    go,
 ):
     rows, span, width = x_ref.shape
     total = chans * span
@@ -70,24 +75,31 @@
     c = lax.axis_index("chan")
     hi = r // group
     lo = r % group
-    is_home = (hi == c).astype(jnp.int32)
     step = 4 if rows % 4 == 0 else 1
     early = max(rows // 8, 1)
-    last = rows // 4
-
+    middle = min(early + MIDDLE, rows)
+    ahead = scores.shape[0]
+    batch = BATCH
+
+    direct = chans == 2
     barrier = pltpu.get_barrier_semaphore()
-    for d in range(1, chans):
-        pl.semaphore_signal(barrier, inc=1, device_id=(r, (c + d) % chans), device_id_type=MESH)
-    for s in range(chans):
-
-        @pl.when(jnp.logical_or(hi != c, c != s))
-        def _():
-            pl.semaphore_signal(barrier, inc=1, device_id=(c * group + lo, s), device_id_type=MESH)
-
-    for d in range(1, group):
-        pl.semaphore_signal(
-            barrier, inc=1, device_id=(hi * group + (lo + d) % group, c), device_id_type=MESH
-        )
+    for other in range(1, chans):
+
+        @pl.when(c == 0)
+        def _():
+            pl.semaphore_signal(barrier, inc=1, device_id=(r, other), device_id_type=MESH)
+
+    for d in range(group):
+
+        @pl.when(jnp.logical_or(c > 0, d > 0))
+        def _():
+            pl.semaphore_signal(
+                barrier, inc=1, device_id=(hi * group + (lo + d) % group, 0), device_id_type=MESH
+            )
+
+    @pl.when(c != hi)
+    def _():
+        pl.semaphore_signal(barrier, inc=1, device_id=(c * group + lo, 0), device_id_type=MESH)
 
     loads = [
         pltpu.make_async_copy(source, target, load_sem.at[k])
@@ -123,14 +135,12 @@
         high = (centered * lax.rsqrt(variance + 1e-05) * gain + shift).astype(jnp.bfloat16)
         for m in range(count):
             xall[first + m, c] = high[m]
-        both = lax.dot_general(
-            bw_both,
-            high.reshape(count * span, width),
-            NT,
-            preferred_element_type=jnp.float32,
-        )
+        return high.reshape(count * span, width)
+
+    def own_bias_rows(first, high):
+        both = lax.dot_general(bw_both, high, NT, preferred_element_type=jnp.float32)
         local = both[:HEADS] + both[HEADS:]
-        for m in range(count):
+        for m in range(high.shape[0] // span):
             stage[:, first + m, :] = local[:, m * span : (m + 1) * span]
 
     def x_copy(i, d, source):
@@ -148,22 +158,53 @@
             x_copy(i, d, c).start()
         return carry
 
+    @pl.when(c > 0)
+    def _():
+        pl.semaphore_wait(barrier, 1)
+        pl.semaphore_signal(ready, inc=1, device_id=(r, 0), device_id_type=MESH)
+
     with jax.named_scope("norm0"):
         chunks[0].wait()
-        norm_rows(0, early)
-    with jax.named_scope("barrier"):
-        pl.semaphore_wait(barrier, 2 * chans - 1 - is_home + group - 1)
-    lax.fori_loop(0, early, send_row, 0)
+        first_rows = norm_rows(0, early)
+    if direct:
+
+        @pl.when(c > 0)
+        def _():
+            lax.fori_loop(0, early, send_row, 0)
 
     with jax.named_scope("norm1"):
         chunks[1].wait()
+        own_bias_rows(0, first_rows)
         for first in range(early, rows, early):
-            norm_rows(first, min(early, rows - first))
+            own_bias_rows(first, norm_rows(first, min(early, rows - first)))
         own_bias[...] = stage[...].astype(jnp.bfloat16)
 
         @pl.when(hi == c)
         def _():
             blocks[lo, c] = stage[...].astype(jnp.bfloat16)
+
+    with jax.named_scope("partner"):
+
+        @pl.when(c == 0)
+        def _():
+            pl.semaphore_wait(ready, chans - 1)
+            if direct:
+                lax.fori_loop(0, early, send_row, 0)
+
+    if direct:
+        lax.fori_loop(early, middle, send_row, 0)
+
+    with jax.named_scope("barrier"):
+
+        @pl.when(c == 0)
+        def _():
+            pl.semaphore_wait(barrier, group * chans - 1 + chans - 1)
+            for other in range(1, chans):
+                pl.semaphore_signal(go, inc=1, device_id=(r, other), device_id_type=MESH)
+
+        @pl.when(c > 0)
+        def _():
+            pl.semaphore_wait(go, 1)
 
     def far_copy(g, source):
         return pltpu.make_async_remote_copy(
@@ -196,7 +237,7 @@
         for d in range(1, group):
             near_copy(d, lo, c).start()
 
-    lax.fori_loop(early, rows, send_row, 0)
+    lax.fori_loop(middle if direct else 0, rows, send_row, 0)
 
     loads[3].wait()
     loads[4].wait()
@@ -238,23 +279,40 @@
                 for d in range(1, group):
                     near_copy(d, lo, part).start()
 
-    def project_other(i):
+    tall = (HEADS * span, width)
+    lane = lax.broadcasted_iota(jnp.int32, (span, width), 1) // head_dim
+    own_lane = lax.broadcasted_iota(jnp.int32, tall, 1) // head_dim
+    own_head = lax.broadcasted_iota(jnp.int32, tall, 0) // span
+
+    def project_other(first, count):
+        here = slice(first, first + count)
         for d in range(1, chans):
             source = (c + chans - d) % chans
-            with jax.named_scope("x_wait"):
+            for i in range(first, first + count):
                 x_copy(i, d, source).wait_recv()
-            other = xall[i, source]
+            other = xall[here, source].reshape(count * span, width)
             kv = jnp.dot(
                 jnp.concatenate([other, other], axis=1),
                 w_own[:, width : 3 * width],
                 preferred_element_type=jnp.float32,
             )
-            keys[i, source] = kv[:, :width].astype(jnp.bfloat16)
-            values[i, source] = kv[:, width:].astype(jnp.bfloat16)
-
-    with jax.named_scope("kv_first"):
-        for i in range(min(4, rows - last)):
-            project_other(i)
+            shape = (count, span, width)
+            keys[here, source] = kv[:, :width].astype(jnp.bfloat16).reshape(shape)
+            values[here, source] = kv[:, width:].astype(jnp.bfloat16).reshape(shape)
+
+    def raw_score(i):
+        mine = jnp.concatenate([queries[i]] * HEADS, axis=0)
+        mine = jnp.where(own_lane == own_head, mine, jnp.zeros_like(mine))
+        return lax.dot_general(
+            mine, keys[i].reshape(total, width), NT, preferred_element_type=jnp.float32
+        )
+
+    with jax.named_scope("ahead"):
+        for first in range(0, ahead, batch):
+            count = min(batch, ahead - first)
+            project_other(first, count)
+            for i in range(first, first + count):
+                scores[i] = raw_score(i)
 
     with jax.named_scope("near_wait"):
         for d in range(1, group):
@@ -271,24 +329,15 @@
                     span, span
                 )
 
-    tall = (HEADS * span, width)
-    lane = lax.broadcasted_iota(jnp.int32, (span, width), 1) // head_dim
-    own_lane = lax.broadcasted_iota(jnp.int32, tall, 1) // head_dim
-    own_head = lax.broadcasted_iota(jnp.int32, tall, 0) // span
-
-    def score(i, slot):
-        mine = jnp.concatenate([queries[i]] * HEADS, axis=0)
-        mine = jnp.where(own_lane == own_head, mine, jnp.zeros_like(mine))
-        part = lax.dot_general(
-            mine, keys[i].reshape(total, width), NT, preferred_element_type=jnp.float32
-        )
+    def score(i):
+        part = scores[i] if i < ahead else raw_score(i)
         part = part + bias[...].reshape(HEADS * span, total)
-        scores[slot] = part
-        peaks[slot] = jnp.broadcast_to(jnp.max(part, axis=-1, keepdims=True), tall)
-
-    def attend(i, slot):
-        peak = jnp.concatenate([peaks[slot]] * (total // width), axis=1)
-        weights = jnp.exp2(scores[slot] - peak).astype(jnp.bfloat16)
+        scores[i % ahead] = part
+        peaks[i % ahead] = jnp.broadcast_to(jnp.max(part, axis=-1, keepdims=True), tall)
+
+    def attend(i):
+        peak = jnp.concatenate([peaks[i % ahead]] * (total // width), axis=1)
+        weights = jnp.exp2(scores[i % ahead] - peak).astype(jnp.bfloat16)
         value = jnp.concatenate(
             [values[i].reshape(total, width), jnp.ones((total, width), jnp.bfloat16)], axis=1
         )
@@ -299,54 +348,23 @@
             here = slice(h * span, (h + 1) * span)
             top = jnp.where(lane == h, both[here, :width], top)
             norm = jnp.where(lane == h, both[here, width:], norm)
-        gated[slot] = (gates[i] * (top / norm)).astype(jnp.bfloat16)
-
-    def finish_row(i, slot):
-        mine = gated[slot]
+        gated[i % 4] = (gates[i] * (top / norm)).astype(jnp.bfloat16)
+
+    def finish_row(i):
+        mine = gated[i % 4]
         out_ref[i] = jnp.dot(
             jnp.concatenate([mine, mine], axis=1), w_out[...], preferred_element_type=jnp.float32
         )
 
-    body = rows - last
-    pairs = [list(range(n, min(n + 2, body))) for n in range(0, body, 2)]
-
-    def slot(i):
-        return i % 4
-
-    with jax.named_scope("score0"):
-        for i in pairs[0]:
-            score(i, slot(i))
-    for n, pair in enumerate(pairs):
-        with jax.named_scope(f"pair{n}"):
-            if n + 2 < len(pairs):
-                for i in pairs[n + 2]:
-                    project_other(i)
-            for u, i in enumerate(pair):
-                if n > 0:
-                    finish_row(pairs[n - 1][u], slot(pairs[n - 1][u]))
-                if n + 1 < len(pairs) and u < len(pairs[n + 1]):
-                    score(pairs[n + 1][u], slot(pairs[n + 1][u]))
-                attend(i, slot(i))
-    pending = list(pairs[-1])
-    waiting = None
-    for i in range(body, rows):
-        with jax.named_scope(f"row{i}"):
-            project_other(i)
-            score(i, slot(i))
-            for k in pending:
-                finish_row(k, slot(k))
-            pending = []
-            if waiting is not None:
-                attend(waiting, slot(waiting))
-                pending = [waiting]
-            waiting = i
-    with jax.named_scope("tail"):
-        for k in pending:
-            finish_row(k, slot(k))
-        attend(waiting, slot(waiting))
-        finish_row(waiting, slot(waiting))
-
-    with jax.named_scope("finish"):
+    pairs = [list(range(n, min(n + 2, rows))) for n in range(0, rows, 2)]
+    sent_early = rows // 2
+
+    def sent(i, carry):
+        for d in range(1, chans):
+            x_copy(i, d, c).wait_send()
+        return carry
+
+    def sent_before():
         for g in range(chans):
 
             @pl.when(jnp.logical_or(hi != c, hi != g))
@@ -356,13 +374,31 @@
         for d in range(1, group):
             for part in range(chans):
                 near_copy(d, lo, part).wait_send()
-
-        def sent(i, carry):
-            for d in range(1, chans):
-                x_copy(i, d, c).wait_send()
-            return carry
-
-        lax.fori_loop(0, rows, sent, 0)
+        lax.fori_loop(0, sent_early, sent, 0)
+
+    with jax.named_scope("score0"):
+        for i in pairs[0]:
+            score(i)
+    for n, pair in enumerate(pairs):
+        with jax.named_scope(f"pair{n}"):
+            after = pairs[n + 1] if n + 1 < len(pairs) else []
+            before = pairs[n - 1] if n > 0 else []
+            if after and after[-1] >= ahead:
+                if n + 2 == len(pairs):
+                    sent_before()
+                project_other(after[0], len(after))
+            for u, i in enumerate(pair):
+                if u < len(before):
+                    finish_row(before[u])
+                if u < len(after):
+                    score(after[u])
+                attend(i)
+    with jax.named_scope("tail"):
+        for i in pairs[-1]:
+            finish_row(i)
+
+    with jax.named_scope("finish"):
+        lax.fori_loop(sent_early, rows, sent, 0)
 
 
 def body(
@@ -379,6 +415,7 @@
     rows, span, width = pair_rep.shape
     group = span // rows
     total = chans * span
+    ahead = max(rows // 8, 1) * AHEAD
     half = jnp.bfloat16
     full = jnp.float32
     return pl.pallas_call(
@@ -406,8 +443,8 @@
             pltpu.VMEM((rows, span, width), full),
             pltpu.VMEM((rows, chans, span, width), half),
             pltpu.VMEM((rows, chans, span, width), half),
-            pltpu.VMEM((4, HEADS * span, total), full),
-            pltpu.VMEM((4, HEADS * span, width), full),
+            pltpu.VMEM((ahead, HEADS * span, total), full),
+            pltpu.VMEM((ahead, HEADS * span, width), full),
             pltpu.VMEM((4, span, width), half),
             pltpu.SemaphoreType.DMA((7,)),
             pltpu.SemaphoreType.DMA((2,)),
@@ -417,6 +454,8 @@
             pltpu.SemaphoreType.DMA((chans,)),
             pltpu.SemaphoreType.DMA((group - 1, chans)),
             pltpu.SemaphoreType.DMA((group - 1, chans)),
+            pltpu.SemaphoreType.REGULAR,
+            pltpu.SemaphoreType.REGULAR,
         ],
         compiler_params=pltpu.CompilerParams(
             collective_id=0, has_side_effects=True, vmem_limit_bytes=(16 + 6 * chans) * 1024 * 1024

time: 21.4 us -> 19.6 us (0.916)
  Pallas kernels: 20.3 us -> 18.5 us
    pallas_call x1, Pallas kernels: 20.3 us -> 18.5 us  [body(): pl.pallas_call(functools.partial(kernel, chans, group), out_shape=jax.Sha...]
where the time goes in v2:
time: 19.6 us; the launch traced here: 19.4 us
  Pallas kernels  18.5 us (94%)
  local copies, waits for them, and re-layouts  0.97 us (5%)
    pallas_call x1, Pallas kernels, body(): pl.pallas_call(functools.partial(kernel, chans, group), out_shape=jax.Sha...  18.5 us
    unnamed x1, local copies, waits for them, and re-layouts  0.97 us

profile of v2, /device:TPU:0, one launch (start us, length us, event | category | flops | bytes accessed | tf_op | source)
XLA Modules:
  0.0 19.4 jit_solution(2188939740990669980)
XLA Ops:
  0.0 18.5 %shard_map.82 = f32[16,128,128]{2,1,0:T(8,128)S(1)} custom-call(f32[16,128,128]{2,1,0:T(8,128)} %x_hbm.1, s32[1,256]{1,0:T(1,128)} %bitcast.6, f32[1,128]{1,0:T(1,128)} %bitcast.7, f32[1,128]{1,0:T(1,128)} %bitcast.8, f32[128,512]{1,0:T(8,128)} %proj_hbm.1, f32[1,128]{1,0:T(1,128)} %bitcast.9, f32[4,128]{1,0:T(4,128)} %bitcast.5, f32[128,128]{1,0:T(8,128)} %ow_hbm.1), custom_call_target="tpu_custom_call" | custom-call | tf_op jit(solution)/shard_map/pallas_call | solution.py:421
  18.5 1.0 %copy.10 = f32[16,128,128]{2,1,0:T(8,128)} copy(f32[16,128,128]{2,1,0:T(8,128)S(1)} %shard_map.82) | data formatting | bytes 2097152

commit v3 on v2

--- a/solution.py
+++ b/solution.py
@@ -9,9 +9,13 @@
 from jax.sharding import PartitionSpec as P
 
 HEADS = 4
-MIDDLE = 3
+ALONE = 2
+EARLY = 2
+LATE = 2
+LATER = 1
+MIDDLE = 4
 BATCH = 2
-AHEAD = 5
+AHEAD = 4
 MESH = pl.DeviceIdType.MESH
 NT = (((1,), (1,)), ((), ()))
 NEVER = -1e30
@@ -39,10 +43,9 @@
     mask_ref,
     gain_ref,
     shift_ref,
-    proj_ref,
+    dense_ref,
     gate_ref,
     bw_ref,
-    ow_ref,
     xall,
     blocks,
     stage,
@@ -58,6 +61,7 @@
     peaks,
     gated,
     load_sem,
+    dense_sem,
     chunk_sem,
     x_send,
     x_recv,
@@ -73,33 +77,14 @@
     head_dim = width // HEADS
     r = lax.axis_index("row")
     c = lax.axis_index("chan")
-    hi = r // group
-    lo = r % group
+    hi = lax.div(r, group)
+    lo = lax.rem(r, group)
     step = 4 if rows % 4 == 0 else 1
-    early = max(rows // 8, 1)
-    middle = min(early + MIDDLE, rows)
+    early = min(EARLY, rows)
+    middle = jnp.where(lax.rem(r, 2) == 0, min(early + MIDDLE, rows), LATE + LATER)
+    first = jnp.where(lax.rem(r, 2) == 0, early, LATE)
     ahead = scores.shape[0]
     batch = BATCH
-
-    direct = chans == 2
-    barrier = pltpu.get_barrier_semaphore()
-    for other in range(1, chans):
-
-        @pl.when(c == 0)
-        def _():
-            pl.semaphore_signal(barrier, inc=1, device_id=(r, other), device_id_type=MESH)
-
-    for d in range(group):
-
-        @pl.when(jnp.logical_or(c > 0, d > 0))
-        def _():
-            pl.semaphore_signal(
-                barrier, inc=1, device_id=(hi * group + (lo + d) % group, 0), device_id_type=MESH
-            )
-
-    @pl.when(c != hi)
-    def _():
-        pl.semaphore_signal(barrier, inc=1, device_id=(c * group + lo, 0), device_id_type=MESH)
 
     loads = [
         pltpu.make_async_copy(source, target, load_sem.at[k])
@@ -108,20 +93,46 @@
                 (gain_hbm, gain_ref),
                 (shift_hbm, shift_ref),
                 (bw_hbm, bw_ref),
-                (proj_hbm, proj_ref),
                 (gate_hbm, gate_ref),
-                (ow_hbm, ow_ref),
                 (mask_hbm, mask_ref),
             ]
         )
+    ]
+    dense = [
+        pltpu.make_async_copy(proj_hbm, dense_ref.at[:, pl.ds(0, 4 * width)], dense_sem),
+        pltpu.make_async_copy(ow_hbm, dense_ref.at[:, pl.ds(4 * width, width)], dense_sem),
     ]
     spans = (pl.ds(0, early), pl.ds(early, rows - early))
     chunks = [
         pltpu.make_async_copy(x_hbm.at[here], x_ref.at[here], chunk_sem.at[k])
         for k, here in enumerate(spans)
     ]
-    for copy in loads[:3] + chunks + loads[3:]:
+    for copy in chunks[:1] + loads[:3]:
         copy.start()
+
+    direct = chans == 2
+    barrier = pltpu.get_barrier_semaphore()
+    for other in range(1, chans):
+
+        @pl.when(c == 0)
+        def _():
+            pl.semaphore_signal(barrier, inc=1, device_id=(r, other), device_id_type=MESH)
+
+    for d in range(group):
+
+        @pl.when(jnp.logical_or(c > 0, d > 0))
+        def _():
+            pl.semaphore_signal(
+                barrier, inc=1, device_id=(hi * group + lax.rem(lo + d, group), 0), device_id_type=MESH
+            )
+
+    @pl.when(c != hi)
+    def _():
+        pl.semaphore_signal(barrier, inc=1, device_id=(c * group + lo, 0), device_id_type=MESH)
+
+    for copy in chunks[1:] + dense + loads[3:]:
+        copy.start()
+
     for copy in loads[:3]:
         copy.wait()
     gain = gain_ref[...].reshape(1, 1, width)
@@ -143,13 +154,28 @@
         for m in range(high.shape[0] // span):
             stage[:, first + m, :] = local[:, m * span : (m + 1) * span]
 
+    alone = max(rows - ALONE, 0) // 2 * 2
+
+    def unit_of(i):
+        return jnp.where(i < alone, i // 2, i - alone + alone // 2)
+
+    def x_rows(here, d, source, unit):
+        return pltpu.make_async_remote_copy(
+            src_ref=xall.at[here, source],
+            dst_ref=xall.at[here, source],
+            send_sem=x_send.at[d - 1],
+            recv_sem=x_recv.at[d - 1, unit],
+            device_id=(r, lax.rem(c + d, chans)),
+            device_id_type=MESH,
+        )
+
     def x_copy(i, d, source):
         return pltpu.make_async_remote_copy(
             src_ref=xall.at[i, source],
             dst_ref=xall.at[i, source],
-            send_sem=x_send.at[d - 1, i],
-            recv_sem=x_recv.at[d - 1, i],
-            device_id=(r, (c + d) % chans),
+            send_sem=x_send.at[d - 1],
+            recv_sem=x_recv.at[d - 1, unit_of(i)],
+            device_id=(r, lax.rem(c + d, chans)),
             device_id_type=MESH,
         )
 
@@ -170,13 +196,13 @@
 
         @pl.when(c > 0)
         def _():
-            lax.fori_loop(0, early, send_row, 0)
+            lax.fori_loop(0, first, send_row, 0)
 
     with jax.named_scope("norm1"):
         chunks[1].wait()
         own_bias_rows(0, first_rows)
-        for first in range(early, rows, early):
-            own_bias_rows(first, norm_rows(first, min(early, rows - first)))
+        for i in range(early, rows, 2):
+            own_bias_rows(i, norm_rows(i, min(2, rows - i)))
         own_bias[...] = stage[...].astype(jnp.bfloat16)
 
         @pl.when(hi == c)
@@ -189,46 +215,76 @@
         def _():
             pl.semaphore_wait(ready, chans - 1)
             if direct:
-                lax.fori_loop(0, early, send_row, 0)
-
-    if direct:
-        lax.fori_loop(early, middle, send_row, 0)
-
-    with jax.named_scope("barrier"):
-
-        @pl.when(c == 0)
-        def _():
-            pl.semaphore_wait(barrier, group * chans - 1 + chans - 1)
-            for other in range(1, chans):
-                pl.semaphore_signal(go, inc=1, device_id=(r, other), device_id_type=MESH)
-
-        @pl.when(c > 0)
-        def _():
-            pl.semaphore_wait(go, 1)
+                lax.fori_loop(0, first, send_row, 0)
 
     def far_copy(g, source):
         return pltpu.make_async_remote_copy(
             src_ref=own_bias,
             dst_ref=blocks.at[lo, source],
-            send_sem=far_send.at[g],
+            send_sem=far_send,
             recv_sem=far_recv.at[source],
             device_id=(g * group + lo, hi),
             device_id_type=MESH,
         )
 
+    if direct:
+
+        @pl.when(hi != c)
+        def _():
+            far_copy(hi, c).start()
+
+    if direct:
+        lax.fori_loop(first, middle, send_row, 0)
+
+    with jax.named_scope("barrier"):
+
+        @pl.when(c == 0)
+        def _():
+            pl.semaphore_wait(barrier, group * chans - 1 + chans - 1)
+            for other in range(1, chans):
+                pl.semaphore_signal(go, inc=1, device_id=(r, other), device_id_type=MESH)
+
+        @pl.when(c > 0)
+        def _():
+            pl.semaphore_wait(go, 1)
+
     for g in range(chans):
-
-        @pl.when(jnp.logical_or(hi != c, hi != g))
+        want = hi != g
+        if not direct:
+            want = jnp.logical_or(want, hi != c)
+
+        @pl.when(want)
         def _():
             far_copy(g, c).start()
+
+    def far_sent(ref):
+        return pltpu.make_async_remote_copy(
+            src_ref=ref,
+            dst_ref=ref,
+            send_sem=far_send,
+            recv_sem=far_recv.at[0],
+            device_id=(hi * group + lax.rem(lo + 1, group), c),
+            device_id_type=MESH,
+        )
+
+    def near_all():
+        every = blocks.at[pl.ds(0, group - 1)]
+        return pltpu.make_async_remote_copy(
+            src_ref=every,
+            dst_ref=every,
+            send_sem=near_send,
+            recv_sem=near_recv,
+            device_id=(hi * group + lax.rem(lo + 1, group), c),
+            device_id_type=MESH,
+        )
 
     def near_copy(d, source, part):
         return pltpu.make_async_remote_copy(
             src_ref=blocks.at[source, part],
             dst_ref=blocks.at[source, part],
-            send_sem=near_send.at[d - 1, part],
-            recv_sem=near_recv.at[d - 1, part],
-            device_id=(hi * group + (lo + d) % group, c),
+            send_sem=near_send,
+            recv_sem=near_recv,
+            device_id=(hi * group + lax.rem(lo + d, group), c),
             device_id_type=MESH,
         )
 
@@ -240,8 +296,8 @@
     lax.fori_loop(middle if direct else 0, rows, send_row, 0)
 
     loads[3].wait()
-    loads[4].wait()
-    proj_high, proj_low = halves(proj_ref[...])
+    pltpu.make_async_copy(dense_ref, dense_ref, dense_sem).wait()
+    proj_high, proj_low = halves(dense_ref[:, : 4 * width])
     w_own[:width] = proj_high
     w_own[width:] = proj_low
     scaling = LOG2E / math.sqrt(head_dim)
@@ -263,15 +319,14 @@
     with jax.named_scope("project_own"):
         lax.fori_loop(0, rows // step, project_own, 0)
 
-    loads[5].wait()
-    loads[6].wait()
-    out_high, out_low = halves(ow_ref[...])
+    loads[4].wait()
+    out_high, out_low = halves(dense_ref[:, 4 * width :])
     w_out[:width] = out_high
     w_out[width:] = out_low
 
     with jax.named_scope("far_wait"):
         for k in range(chans):
-            part = (c + k) % chans
+            part = lax.rem(c + k, chans)
 
             @pl.when(jnp.logical_or(hi != c, k > 0))
             def _():
@@ -287,9 +342,9 @@
     def project_other(first, count):
         here = slice(first, first + count)
         for d in range(1, chans):
-            source = (c + chans - d) % chans
-            for i in range(first, first + count):
-                x_copy(i, d, source).wait_recv()
+            source = lax.rem(c + chans - d, chans)
+            unit = first // 2 if first < alone else first - alone + alone // 2
+            x_rows(pl.ds(first, count), d, source, unit).wait_recv()
             other = xall[here, source].reshape(count * span, width)
             kv = jnp.dot(
                 jnp.concatenate([other, other], axis=1),
@@ -308,16 +363,14 @@
         )
 
     with jax.named_scope("ahead"):
-        for first in range(0, ahead, batch):
-            count = min(batch, ahead - first)
-            project_other(first, count)
-            for i in range(first, first + count):
+        for start in range(0, ahead, batch):
+            count = min(batch, ahead - start)
+            project_other(start, count)
+            for i in range(start, start + count):
                 scores[i] = raw_score(i)
 
     with jax.named_scope("near_wait"):
-        for d in range(1, group):
-            for part in range(chans):
-                near_copy(d, (lo + group - d) % group, part).wait_recv()
+        near_all().wait_recv()
 
     with jax.named_scope("bias_prep"):
         valid = mask_ref[...] > 0
@@ -356,25 +409,18 @@
             jnp.concatenate([mine, mine], axis=1), w_out[...], preferred_element_type=jnp.float32
         )
 
-    pairs = [list(range(n, min(n + 2, rows))) for n in range(0, rows, 2)]
-    sent_early = rows // 2
-
-    def sent(i, carry):
-        for d in range(1, chans):
-            x_copy(i, d, c).wait_send()
-        return carry
-
+    pairs = [list(range(n, min(n + 2, alone))) for n in range(0, alone, 2)]
+    pairs += [[i] for i in range(alone, rows)]
     def sent_before():
-        for g in range(chans):
-
-            @pl.when(jnp.logical_or(hi != c, hi != g))
-            def _():
-                far_copy(g, c).wait_send()
-
-        for d in range(1, group):
-            for part in range(chans):
-                near_copy(d, lo, part).wait_send()
-        lax.fori_loop(0, sent_early, sent, 0)
+        @pl.when(hi == c)
+        def _():
+            far_sent(own_bias if chans == 2 else blocks.at[0, pl.ds(0, chans - 1)]).wait_send()
+
+        @pl.when(hi != c)
+        def _():
+            far_sent(blocks.at[0]).wait_send()
+
+        near_all().wait_send()
 
     with jax.named_scope("score0"):
         for i in pairs[0]:
@@ -387,18 +433,20 @@
                 if n + 2 == len(pairs):
                     sent_before()
                 project_other(after[0], len(after))
-            for u, i in enumerate(pair):
+            for u in range(max(len(before), len(after), len(pair))):
                 if u < len(before):
                     finish_row(before[u])
                 if u < len(after):
                     score(after[u])
-                attend(i)
+                if u < len(pair):
+                    attend(pair[u])
     with jax.named_scope("tail"):
         for i in pairs[-1]:
             finish_row(i)
 
     with jax.named_scope("finish"):
-        lax.fori_loop(sent_early, rows, sent, 0)
+        for d in range(1, chans):
+            x_rows(pl.ds(0, rows), d, c, 0).wait_send()
 
 
 def body(
@@ -416,6 +464,7 @@
     group = span // rows
     total = chans * span
     ahead = max(rows // 8, 1) * AHEAD
+    alone = max(rows - ALONE, 0) // 2 * 2
     half = jnp.bfloat16
     full = jnp.float32
     return pl.pallas_call(
@@ -428,10 +477,9 @@
             pltpu.VMEM((1, total), jnp.int32),
             pltpu.VMEM((1, width), full),
             pltpu.VMEM((1, width), full),
-            pltpu.VMEM((width, 4 * width), full),
+            pltpu.VMEM((width, 5 * width), full),
             pltpu.VMEM((1, width), full),
             pltpu.VMEM((HEADS, width), full),
-            pltpu.VMEM((width, width), full),
             pltpu.VMEM((rows, chans, span, width), half),
             pltpu.VMEM((group, chans, HEADS, rows, span), half),
             pltpu.VMEM((HEADS, rows, span), full),
@@ -446,14 +494,15 @@
             pltpu.VMEM((ahead, HEADS * span, total), full),
             pltpu.VMEM((ahead, HEADS * span, width), full),
             pltpu.VMEM((4, span, width), half),
-            pltpu.SemaphoreType.DMA((7,)),
+            pltpu.SemaphoreType.DMA((5,)),
+            pltpu.SemaphoreType.DMA,
             pltpu.SemaphoreType.DMA((2,)),
-            pltpu.SemaphoreType.DMA((chans - 1, rows)),
-            pltpu.SemaphoreType.DMA((chans - 1, rows)),
+            pltpu.SemaphoreType.DMA((chans - 1,)),
+            pltpu.SemaphoreType.DMA((chans - 1, alone // 2 + rows - alone)),
+            pltpu.SemaphoreType.DMA,
             pltpu.SemaphoreType.DMA((chans,)),
-            pltpu.SemaphoreType.DMA((chans,)),
-            pltpu.SemaphoreType.DMA((group - 1, chans)),
-            pltpu.SemaphoreType.DMA((group - 1, chans)),
+            pltpu.SemaphoreType.DMA,
+            pltpu.SemaphoreType.DMA,
             pltpu.SemaphoreType.REGULAR,
             pltpu.SemaphoreType.REGULAR,
         ],

time: 19.6 us -> 18.5 us (0.944)
  Pallas kernels: 18.5 us -> 17.4 us
    pallas_call x1, Pallas kernels: 18.5 us -> 17.4 us  [body(): pl.pallas_call(functools.partial(kernel, chans, group), out_shape=jax.Sha...]
where the time goes in v3:
time: 18.5 us; the launch traced here: 18.4 us
  Pallas kernels  17.4 us (94%)
  local copies, waits for them, and re-layouts  0.97 us (5%)
    pallas_call x1, Pallas kernels, body(): pl.pallas_call(functools.partial(kernel, chans, group), out_shape=jax.Sha...  17.4 us
    unnamed x1, local copies, waits for them, and re-layouts  0.97 us

profile of v3, /device:TPU:0, one launch (start us, length us, event | category | flops | bytes accessed | tf_op | source)
XLA Modules:
  0.0 18.4 jit_solution(16700632968445230596)
XLA Ops:
  0.0 17.4 %shard_map.82 = f32[16,128,128]{2,1,0:T(8,128)S(1)} custom-call(f32[16,128,128]{2,1,0:T(8,128)} %x_hbm.1, s32[1,256]{1,0:T(1,128)} %bitcast.6, f32[1,128]{1,0:T(1,128)} %bitcast.7, f32[1,128]{1,0:T(1,128)} %bitcast.8, f32[128,512]{1,0:T(8,128)} %proj_hbm.1, f32[1,128]{1,0:T(1,128)} %bitcast.9, f32[4,128]{1,0:T(4,128)} %bitcast.5, f32[128,128]{1,0:T(8,128)} %ow_hbm.1), custom_call_target="tpu_custom_call" | custom-call | tf_op jit(solution)/shard_map/pallas_call | solution.py:470
  17.4 1.0 %copy.10 = f32[16,128,128]{2,1,0:T(8,128)} copy(f32[16,128,128]{2,1,0:T(8,128)S(1)} %shard_map.82) | data formatting | bytes 2097152

commit v4 on v3

--- a/solution.py
+++ b/solution.py
@@ -15,7 +15,7 @@
 LATER = 1
 MIDDLE = 4
 BATCH = 2
-AHEAD = 4
+AHEAD = 5
 MESH = pl.DeviceIdType.MESH
 NT = (((1,), (1,)), ((), ()))
 NEVER = -1e30
@@ -70,7 +70,6 @@
     near_send,
     near_recv,
     ready,
-    go,
 ):
     rows, span, width = x_ref.shape
     total = chans * span
@@ -242,20 +241,31 @@
         def _():
             pl.semaphore_wait(barrier, group * chans - 1 + chans - 1)
             for other in range(1, chans):
-                pl.semaphore_signal(go, inc=1, device_id=(r, other), device_id_type=MESH)
+                pl.semaphore_signal(ready, inc=1, device_id=(r, other), device_id_type=MESH)
 
         @pl.when(c > 0)
         def _():
-            pl.semaphore_wait(go, 1)
+            pl.semaphore_wait(ready, 1)
 
     for g in range(chans):
-        want = hi != g
-        if not direct:
-            want = jnp.logical_or(want, hi != c)
+        if direct:
+            want = jnp.logical_and(hi != g, c <= hi)
+        else:
+            want = jnp.logical_or(hi != g, hi != c)
 
         @pl.when(want)
         def _():
             far_copy(g, c).start()
+
+    def relay(g, part):
+        return pltpu.make_async_remote_copy(
+            src_ref=blocks.at[lo, part],
+            dst_ref=blocks.at[lo, part],
+            send_sem=far_send,
+            recv_sem=far_recv.at[part],
+            device_id=(g * group + lo, c),
+            device_id_type=MESH,
+        )
 
     def far_sent(ref):
         return pltpu.make_async_remote_copy(
@@ -331,6 +341,12 @@
             @pl.when(jnp.logical_or(hi != c, k > 0))
             def _():
                 far_copy(part, part).wait_recv()
+                if direct and k > 0:
+
+                    @pl.when(jnp.logical_and(c == 0, hi == 0))
+                    def _():
+                        relay(1, part).start()
+
                 for d in range(1, group):
                     near_copy(d, lo, part).start()
 
@@ -412,11 +428,17 @@
     pairs = [list(range(n, min(n + 2, alone))) for n in range(0, alone, 2)]
     pairs += [[i] for i in range(alone, rows)]
     def sent_before():
-        @pl.when(hi == c)
-        def _():
-            far_sent(own_bias if chans == 2 else blocks.at[0, pl.ds(0, chans - 1)]).wait_send()
-
-        @pl.when(hi != c)
+        if direct:
+            single = c > 0
+        else:
+            single = hi == c
+        few = own_bias if chans == 2 else blocks.at[0, pl.ds(0, chans - 1)]
+
+        @pl.when(single)
+        def _():
+            far_sent(few).wait_send()
+
+        @pl.when(jnp.logical_not(single))
         def _():
             far_sent(blocks.at[0]).wait_send()
 
@@ -429,7 +451,8 @@
         with jax.named_scope(f"pair{n}"):
             after = pairs[n + 1] if n + 1 < len(pairs) else []
             before = pairs[n - 1] if n > 0 else []
-            if after and after[-1] >= ahead:
+            coming = pairs[n + 2] if n + 2 < len(pairs) else []
+            if after and after[-1] >= alone:
                 if n + 2 == len(pairs):
                     sent_before()
                 project_other(after[0], len(after))
@@ -440,6 +463,8 @@
                     score(after[u])
                 if u < len(pair):
                     attend(pair[u])
+            if coming and coming[-1] >= ahead and coming[-1] < alone:
+                project_other(coming[0], len(coming))
     with jax.named_scope("tail"):
         for i in pairs[-1]:
             finish_row(i)
@@ -504,7 +529,6 @@
             pltpu.SemaphoreType.DMA,
             pltpu.SemaphoreType.DMA,
             pltpu.SemaphoreType.REGULAR,
-            pltpu.SemaphoreType.REGULAR,
         ],
         compiler_params=pltpu.CompilerParams(
             collective_id=0, has_side_effects=True, vmem_limit_bytes=(16 + 6 * chans) * 1024 * 1024

time: 18.5 us -> 18.5 us (level)
  no operation moved by 1% of the time
where the time goes in v4:
time: 18.5 us; the launch traced here: 18.4 us
  Pallas kernels  17.4 us (94%)
  local copies, waits for them, and re-layouts  0.97 us (5%)
    pallas_call x1, Pallas kernels, body(): pl.pallas_call(functools.partial(kernel, chans, group), out_shape=jax.Sha...  17.4 us
    unnamed x1, local copies, waits for them, and re-layouts  0.97 us

profile of v4, /device:TPU:0, one launch (start us, length us, event | category | flops | bytes accessed | tf_op | source)
XLA Modules:
  0.0 18.4 jit_solution(1183331089762729997)
XLA Ops:
  0.0 17.4 %shard_map.82 = f32[16,128,128]{2,1,0:T(8,128)S(1)} custom-call(f32[16,128,128]{2,1,0:T(8,128)} %x_hbm.1, s32[1,256]{1,0:T(1,128)} %bitcast.6, f32[1,128]{1,0:T(1,128)} %bitcast.7, f32[1,128]{1,0:T(1,128)} %bitcast.8, f32[128,512]{1,0:T(8,128)} %proj_hbm.1, f32[1,128]{1,0:T(1,128)} %bitcast.9, f32[4,128]{1,0:T(4,128)} %bitcast.5, f32[128,128]{1,0:T(8,128)} %ow_hbm.1), custom_call_target="tpu_custom_call" | custom-call | tf_op jit(solution)/shard_map/pallas_call | solution.py:495
  17.4 1.0 %copy.10 = f32[16,128,128]{2,1,0:T(8,128)} copy(f32[16,128,128]{2,1,0:T(8,128)S(1)} %shard_map.82) | data formatting | bytes 2097152

commit v5 on v4

--- a/solution.py
+++ b/solution.py
@@ -15,7 +15,7 @@
 LATER = 1
 MIDDLE = 4
 BATCH = 2
-AHEAD = 5
+AHEAD = 4
 MESH = pl.DeviceIdType.MESH
 NT = (((1,), (1,)), ((), ()))
 NEVER = -1e30

time: 18.5 us -> 18.5 us (level)
  no operation moved by 1% of the time
where the time goes in v5:
time: 18.5 us; the launch traced here: 18.4 us
  Pallas kernels  17.4 us (94%)
  local copies, waits for them, and re-layouts  0.97 us (5%)
    pallas_call x1, Pallas kernels, body(): pl.pallas_call(functools.partial(kernel, chans, group), out_shape=jax.Sha...  17.4 us
    unnamed x1, local copies, waits for them, and re-layouts  0.97 us

profile of v5, /device:TPU:0, one launch (start us, length us, event | category | flops | bytes accessed | tf_op | source)
XLA Modules:
  0.0 18.4 jit_solution(1568438875280591833)
XLA Ops:
  0.0 17.4 %shard_map.82 = f32[16,128,128]{2,1,0:T(8,128)S(1)} custom-call(f32[16,128,128]{2,1,0:T(8,128)} %x_hbm.1, s32[1,256]{1,0:T(1,128)} %bitcast.6, f32[1,128]{1,0:T(1,128)} %bitcast.7, f32[1,128]{1,0:T(1,128)} %bitcast.8, f32[128,512]{1,0:T(8,128)} %proj_hbm.1, f32[1,128]{1,0:T(1,128)} %bitcast.9, f32[4,128]{1,0:T(4,128)} %bitcast.5, f32[128,128]{1,0:T(8,128)} %ow_hbm.1), custom_call_target="tpu_custom_call" | custom-call | tf_op jit(solution)/shard_map/pallas_call | solution.py:495
  17.4 1.0 %copy.10 = f32[16,128,128]{2,1,0:T(8,128)} copy(f32[16,128,128]{2,1,0:T(8,128)S(1)} %shard_map.82) | data formatting | bytes 2097152
